TPU v7x, 32 devices: a whole 2x2x4 slice. The times are simulated.
32 devices in a mesh: dp: 2 (over core), wide: 4 (over y, x), narrow: 4 (over z).
Axes of the slice: x: 2, y: 2, z: 4, core: 2. Of those that a mesh axis runs over, the one named last changes fastest.
Arguments:
- block_input: float32 [1600, 4096], P('wide', ('dp', 'narrow')), as said below
- block_cotangent: float32 [1600, 4096], P('wide', ('dp', 'narrow')), may hold values from -6 to 6
- seq_start: int32 [32, 128], P(('dp', 'wide', 'narrow')), may hold values from 0 to 127, as said below
- ln1_gain: float32 [1600], P('wide'), may hold values from 0.5 to 1.5
- ln1_shift: float32 [1600], P('wide'), may hold values from -2 to 2
- w_qkv: float32 [1600, 3, 1600], P('wide', None, 'narrow'), may hold values from -0.15625 to 0.15625
- b_qv: float32 [2, 1600], P(None, 'narrow'), may hold values from -3 to 3
- w_out: float32 [1600, 1600], P('wide', 'narrow'), may hold values from -0.4375 to 0.4375
- b_out: float32 [1600], P('wide'), may hold values from -2 to 2
- ln2_gain: float32 [1600], P('wide'), may hold values from 0.5 to 1.5
- ln2_shift: float32 [1600], P('wide'), may hold values from -2 to 2
- w_fc: float32 [1600, 6400], P('wide', 'narrow'), may hold values from -0.15625 to 0.15625
- b_fc: float32 [6400], P('narrow'), may hold values from -3 to 3
- w_proj: float32 [1600, 6400], P('wide', 'narrow'), may hold values from -0.078125 to 0.078125
- b_proj: float32 [1600], P('wide'), may hold values from -2 to 2
Outputs:
- block_output: float32 [1600, 4096], P('wide', ('dp', 'narrow'))
- input_grad: float32 [1600, 4096], P('wide', ('dp', 'narrow'))
- grad_ln1_gain: float32 [1600], P('wide')
- grad_ln1_shift: float32 [1600], P('wide')
- grad_w_qkv: float32 [1600, 3, 1600], P('wide', None, 'narrow')
- grad_b_qv: float32 [2, 1600], P(None, 'narrow')
- grad_w_out: float32 [1600, 1600], P('wide', 'narrow')
- grad_b_out: float32 [1600], P('wide')
- grad_ln2_gain: float32 [1600], P('wide')
- grad_ln2_shift: float32 [1600], P('wide')
- grad_w_fc: float32 [1600, 6400], P('wide', 'narrow')
- grad_b_fc: float32 [6400], P('narrow')
- grad_w_proj: float32 [1600, 6400], P('wide', 'narrow')
- grad_b_proj: float32 [1600], P('wide')
Inputs may be any that keep to these rules, and one draw needn't show every extreme that they name: `block_input`: token activations of order one, with scales that differ from token to token. `seq_start`: along each row the values never fall; each equals the token's own position at the first token of its sequence and the start of its sequence after it. Block 0 holds one sequence of 128 tokens; some block ends with a sequence of one token.
All inputs are finite; a program needn't handle non-finite values.
Results may differ from a plain program's by a relative error of at most 0.011.
Values may be sent and summed in bfloat16 or wider, within the bound.
A program may use at most 320 MiB of HBM per device.

v0:
```python
import math
import jax
import jax.numpy as jnp
from jax import lax
from jax.sharding import PartitionSpec as P

HEADS = 25
HEAD = 64
EPS = 1e-05
GELU_C = math.sqrt(2.0 / math.pi)
BF = jnp.bfloat16
F32 = jnp.float32


def gelu_value(pre_act):
    inner = GELU_C * (pre_act + 0.044715 * pre_act * pre_act * pre_act)
    return 0.5 * pre_act * (1.0 + jnp.tanh(inner))


def gelu_slope(pre_act):
    tanh_part = jnp.tanh(GELU_C * (pre_act + 0.044715 * pre_act * pre_act * pre_act))
    return 0.5 * (1.0 + tanh_part) + 0.5 * pre_act * (1.0 - tanh_part * tanh_part) * GELU_C * (
        1.0 + 3.0 * 0.044715 * pre_act * pre_act
    )


def dot(a, b, ca, cb):
    return lax.dot_general(a, b, (((ca,), (cb,)), ((), ())), preferred_element_type=F32)


def row_totals(first_term, second_term):
    return lax.psum(
        (jnp.sum(first_term, axis=1, keepdims=True), jnp.sum(second_term, axis=1, keepdims=True)),
        "wide",
    )


def norm_forward(inputs, gain_shard, shift_shard):
    full_width = inputs.shape[1] * lax.axis_size("wide")
    total_sum, square_sum = row_totals(inputs, inputs * inputs)
    mean_row = total_sum / full_width
    inv_std = lax.rsqrt(square_sum / full_width - mean_row * mean_row + EPS)
    normed = (inputs - mean_row) * inv_std
    return (normed, inv_std, (normed * gain_shard + shift_shard).astype(BF))


def norm_backward(row_grads, normed, inv_std, gain_shard):
    full_width = row_grads.shape[1] * lax.axis_size("wide")
    scaled = row_grads * gain_shard
    first_sum, second_sum = row_totals(scaled, scaled * normed)
    return inv_std * (scaled - first_sum / full_width - normed * (second_sum / full_width))


def gather_tokens(values):
    return lax.all_gather(values, "wide", axis=0, tiled=True)


def gather_narrow(values):
    return lax.all_gather(values, "narrow", axis=0, tiled=True)


def sum_tokens(partial_value):
    return lax.psum_scatter(
        partial_value.astype(BF), "wide", scatter_dimension=0, tiled=True
    ).astype(F32)


def sum_narrow(partial_value):
    return lax.psum_scatter(
        partial_value.astype(BF), "narrow", scatter_dimension=0, tiled=True
    ).astype(F32)


def to_tokens(values):
    return lax.all_to_all(values, "wide", split_axis=0, concat_axis=1, tiled=True)


def to_features(values):
    return lax.all_to_all(values, "wide", split_axis=1, concat_axis=0, tiled=True)


def block_mask(starts):
    position = jnp.arange(starts.shape[0])
    return (position[None, :] <= position[:, None]) & (starts[:, None] == starts[None, :])


def split_heads(values):
    return values.reshape(values.shape[0], HEADS, HEAD)


def attend_forward(heads_all, allowed):
    score_scale = 1.0 / math.sqrt(HEAD)
    queries = split_heads(heads_all[:, 0])
    keys_part = split_heads(heads_all[:, 1])
    values_part = split_heads(heads_all[:, 2])
    scores = (
        jnp.einsum("ihd,jhd->hij", queries, keys_part, preferred_element_type=F32) * score_scale
    )
    log_total = jnp.log(jnp.sum(jnp.where(allowed, jnp.exp(scores), 0.0), axis=2, keepdims=True))
    attn_probs = jnp.where(allowed, jnp.exp(scores - log_total), 0.0).astype(BF)
    attended = jnp.einsum("hij,jhd->ihd", attn_probs, values_part, preferred_element_type=F32)
    return (attended.reshape(heads_all.shape[0], HEADS * HEAD).astype(BF), log_total)


def attend_backward(heads_all, allowed, log_total, attended_cot):
    score_scale = 1.0 / math.sqrt(HEAD)
    queries = split_heads(heads_all[:, 0])
    keys_part = split_heads(heads_all[:, 1])
    values_part = split_heads(heads_all[:, 2])
    scores = (
        jnp.einsum("ihd,jhd->hij", queries, keys_part, preferred_element_type=F32) * score_scale
    )
    probs_full = jnp.where(allowed, jnp.exp(scores - log_total), 0.0)
    cot_heads = split_heads(attended_cot)
    dprobs = jnp.einsum("ihd,jhd->hij", cot_heads, values_part, preferred_element_type=F32)
    row_delta = jnp.sum(probs_full * dprobs, axis=2, keepdims=True)
    score_cot = (probs_full * (dprobs - row_delta) * score_scale).astype(BF)
    query_grad = jnp.einsum("hij,jhd->ihd", score_cot, keys_part, preferred_element_type=F32)
    key_grad = jnp.einsum("hij,ihd->jhd", score_cot, queries, preferred_element_type=F32)
    value_grad = jnp.einsum(
        "hij,ihd->jhd", probs_full.astype(BF), cot_heads, preferred_element_type=F32
    )
    stacked = jnp.stack([query_grad, key_grad, value_grad], axis=1)
    return stacked.reshape(heads_all.shape[0], 3, HEADS * HEAD)


def own_half(values, axis):
    half = values.shape[axis] // lax.axis_size("dp")
    return lax.dynamic_slice_in_dim(values, lax.axis_index("dp") * half, half, axis)


def local(
    block_input,
    block_cotangent,
    seq_start,
    ln1_gain,
    ln1_shift,
    w_qkv,
    b_qv,
    w_out,
    b_out,
    ln2_gain,
    ln2_shift,
    w_fc,
    b_fc,
    w_proj,
    b_proj,
):
    cores, wide, narrow = (lax.axis_size("dp"), lax.axis_size("wide"), lax.axis_size("narrow"))
    w_index, n_index = (lax.axis_index("wide"), lax.axis_index("narrow"))
    feats, part = (w_qkv.shape[0], w_qkv.shape[2])
    width = feats * wide
    hid = w_fc.shape[1]
    perm = []
    for w in range(wide):
        for n in range(narrow):
            block = n * wide + w
            perm.append((block, w * narrow + n))
    starts = lax.ppermute(seq_start, ("wide", "narrow"), perm)[0]
    allowed = block_mask(starts)
    wq_mine = own_half(w_qkv.astype(BF).reshape(feats, 3 * part), 0)
    wq_all = lax.all_gather(wq_mine, ("narrow", "dp"), axis=0, tiled=True)
    wq_all = wq_all.reshape(narrow, feats, 3 * part)
    wo_mine = lax.all_gather(own_half(w_out.astype(BF), 0), "narrow", axis=1, tiled=True)
    wo_all = lax.all_gather(wo_mine, ("wide", "dp"), axis=0, tiled=True)
    wf_all = lax.all_gather(own_half(w_fc.astype(BF), 0), ("wide", "dp"), axis=0, tiled=True)
    wp_all = lax.all_gather(own_half(w_proj.astype(BF), 0), ("wide", "dp"), axis=0, tiled=True)
    b_out_full, gain_two_full, shift_two_full = lax.all_gather(
        jnp.stack([b_out, ln2_gain, ln2_shift]), "wide", axis=1, tiled=True
    )
    bias_qv = lax.all_gather(b_qv, "narrow", axis=0).reshape(narrow, 1, 2, part)
    bias_three = jnp.concatenate(
        [bias_qv[:, :, 0], jnp.zeros((narrow, 1, part), F32), bias_qv[:, :, 1]], axis=2
    )
    rows_input = block_input.T
    rows_cot = block_cotangent.T
    x_tok = to_tokens(rows_input)
    dy_tok = to_tokens(rows_cot)
    cot_all = gather_narrow(dy_tok.astype(BF))
    normed_one, inv_one, norm_one = norm_forward(rows_input, ln1_gain, ln1_shift)
    qkv_part = jnp.einsum("tk,nkc->tnc", norm_one, wq_all, preferred_element_type=F32)
    qkv_rows = sum_tokens(qkv_part.transpose(0, 1, 2)).transpose(1, 0, 2)
    qkv_rows = (qkv_rows + bias_three).astype(BF)
    heads_all = qkv_rows.reshape(narrow, -1, 3, part).transpose(1, 2, 0, 3).reshape(-1, 3, width)
    attended, log_total = attend_forward(heads_all, allowed)
    residual = x_tok + dot(attended, wo_all, 1, 1) + b_out_full
    mean_two = jnp.mean(residual, axis=1, keepdims=True)
    inv_two = lax.rsqrt(
        jnp.mean(residual * residual, axis=1, keepdims=True) - mean_two * mean_two + EPS
    )
    normed_two = (residual - mean_two) * inv_two
    norm_two = (normed_two * gain_two_full + shift_two_full).astype(BF)
    norm_two_all = gather_narrow(norm_two)
    pre_act = dot(norm_two_all, wf_all, 1, 0) + b_fc
    hidden = gelu_value(pre_act).astype(BF)
    out_tok = residual + sum_narrow(dot(hidden, wp_all, 1, 1))
    output_rows = to_features(out_tok) + b_proj
    pre_grad = dot(cot_all, wp_all, 1, 0) * gelu_slope(pre_act)
    pre_cot = pre_grad.astype(BF)
    norm_two_grad = sum_narrow(dot(pre_cot, wf_all, 1, 1))

    def reduce_wide(grad):
        total = lax.psum_scatter(grad.astype(BF), ("wide", "dp"), scatter_dimension=0, tiled=True)
        return total

    def share(total):
        return lax.all_gather(total, "dp", axis=0, tiled=True).astype(F32)

    grad_w_proj = share(reduce_wide(dot(cot_all, hidden, 0, 0)))
    grad_w_fc = share(reduce_wide(dot(norm_two_all, pre_cot, 0, 0)))
    scaled = norm_two_grad * gain_two_full
    mean_scaled = jnp.mean(scaled, axis=1, keepdims=True)
    mean_cross = jnp.mean(scaled * normed_two, axis=1, keepdims=True)
    resid_grad = dy_tok + inv_two * (scaled - mean_scaled - normed_two * mean_cross)
    resid_cot = resid_grad.astype(BF)
    attended_cot = dot(resid_cot, wo_all, 1, 0).astype(BF)
    wo_grad = reduce_wide(dot(resid_cot, attended, 0, 0))
    wo_grad = lax.psum_scatter(wo_grad, "narrow", scatter_dimension=1, tiled=True)
    grad_w_out = share(wo_grad)
    qkv_grad = attend_backward(heads_all, allowed, log_total, attended_cot)
    qkv_cot = qkv_grad.astype(BF).reshape(-1, 3, narrow, part).transpose(0, 2, 1, 3)
    qkv_cot_all = gather_tokens(qkv_cot.reshape(-1, narrow, 3 * part))
    norm_one_grad = jnp.einsum("tnc,nkc->tk", qkv_cot_all, wq_all, preferred_element_type=F32)
    wq_grad = jnp.einsum("tk,tnc->nkc", norm_one, qkv_cot_all, preferred_element_type=F32).astype(
        BF
    )
    wq_grad = lax.psum_scatter(
        wq_grad.reshape(narrow * feats, 3 * part), ("narrow", "dp"), scatter_dimension=0, tiled=True
    )
    grad_w_qkv = share(wq_grad).reshape(feats, 3, part)
    resid_back = to_features(resid_grad)
    grad_input_rows = resid_back + norm_backward(norm_one_grad, normed_one, inv_one, ln1_gain)
    qkv_sums = jnp.sum(qkv_grad, axis=0)
    fc_full = lax.dynamic_update_slice_in_dim(
        jnp.zeros((narrow * hid,), F32), jnp.sum(pre_grad, axis=0), n_index * hid, 0
    )
    token_terms = jnp.stack(
        [
            qkv_sums[0],
            qkv_sums[2],
            jnp.sum(resid_grad, axis=0),
            jnp.sum(norm_two_grad * normed_two, axis=0),
            jnp.sum(norm_two_grad, axis=0),
        ]
    )
    feature_terms = jnp.stack(
        [
            jnp.sum(norm_one_grad * normed_one, axis=0),
            jnp.sum(norm_one_grad, axis=0),
            jnp.sum(rows_cot, axis=0),
        ]
    )
    feature_full = lax.dynamic_update_slice_in_dim(
        jnp.zeros((3, width), F32), feature_terms, w_index * feats, 1
    )
    token_sum, feature_sum, fc_sum = lax.psum(
        (token_terms, feature_full, fc_full), ("dp", "wide", "narrow")
    )
    grad_b_qv = lax.dynamic_slice_in_dim(token_sum[:2], n_index * part, part, 1)
    out_bias, gain_two, shift_two = lax.dynamic_slice_in_dim(
        token_sum[2:], w_index * feats, feats, 1
    )
    gain_one, shift_one, proj_bias = lax.dynamic_slice_in_dim(
        feature_sum, w_index * feats, feats, 1
    )
    grad_b_fc = lax.dynamic_slice_in_dim(fc_sum, n_index * hid, hid, 0)
    return (
        output_rows.T,
        grad_input_rows.T,
        gain_one,
        shift_one,
        grad_w_qkv,
        grad_b_qv,
        grad_w_out,
        out_bias,
        gain_two,
        shift_two,
        grad_w_fc,
        grad_b_fc,
        grad_w_proj,
        proj_bias,
    )


def solution(mesh):
    return jax.shard_map(
        local,
        mesh=mesh,
        in_specs=(
            P("wide", ("dp", "narrow")),
            P("wide", ("dp", "narrow")),
            P(("dp", "wide", "narrow"), None),
            P("wide"),
            P("wide"),
            P("wide", None, "narrow"),
            P(None, "narrow"),
            P("wide", "narrow"),
            P("wide"),
            P("wide"),
            P("wide"),
            P("wide", "narrow"),
            P("narrow"),
            P("wide", "narrow"),
            P("wide"),
        ),
        out_specs=(
            P("wide", ("dp", "narrow")),
            P("wide", ("dp", "narrow")),
            P("wide"),
            P("wide"),
            P("wide", None, "narrow"),
            P(None, "narrow"),
            P("wide", "narrow"),
            P("wide"),
            P("wide"),
            P("wide"),
            P("wide", "narrow"),
            P("narrow"),
            P("wide", "narrow"),
            P("wide"),
        ),
        check_vma=False,
    )
```

profile of v0, /device:TPU:9, one launch (start us, length us, event | category | flops | bytes accessed | tf_op | source)
XLA Modules:
  0.0 814.7 jit_solution(4616256458298618883)
XLA Ops:
  8.1 3.0 convert_element_type.104
  18.2 7.9 all-reduce.5
  26.2 38.4 %all-gather.13.cloned.1.call-done = bf16[1600,1200]{1,0:T(8,128)(2,1)} async-done(((bf16[200,1200]{1,0:T(8,128)(2,1)}), bf16[1600,1200]{1,0:T(8,128)(2,1)}) %all-gather.13.cloned.1.call-update) | async-done | bytes 3840016 | tf_op jit(solution)/shard_map/all_gather | solution.py:162
  64.6 8.2 %convolution_convert_fusion.3 = bf16[512,4,1200]{0,2,1:T(8,128)(2,1)} fusion(bf16[4,400,1200]{2,1,0:T(8,128)(2,1)} %bitcast.247, f32[400,512]{1,0:T(8,128)S(1)} %copy-done.2, f32[400]{0:T(512)S(1)} %copy-done.25, f32[400]{0:T(512)S(1)} %copy-done.23, f32[512]{0:T(512)S(1)} %bitcast.228, f32[512]{0:T(512)S(1)} %bitcast.224), kind=kOutput, calls=%fused_computation.6 | convolution fusion | flops 1969561600 | bytes 9581696 | tf_op jit(solution)/shard_map/tk,nkc->tnc/dot_general | solution.py:181
  72.8 7.5 copy.132
  83.8 17.2 %all_gather.48 = bf16[200,1600]{0,1:T(8,128)(2,1)} all-gather(bf16[200,400]{0,1:T(8,128)(2,1)} %copy.136), channel_id=1, replica_groups=mesh['dp'=2,'wide'=4,'narrow'=4] {'narrow'}, dimensions={1}, use_global_device_ids=true | all-gather | bytes 800000 | tf_op jit(solution)/shard_map/all_gather | solution.py:164
  104.4 4.2 collective-permute-start
  109.6 4.2 all-to-all-start
  113.9 22.5 %all-gather.2 = f32[4,400,3]{1,2,0:T(4,128)S(1)} all-gather(f32[1,400,3]{1,2,0:T(4,128)S(1)} %maximum_bitcast_fusion.1), channel_id=1, replica_groups=mesh['dp'=2,'wide'=4,'narrow'=4] {'wide'}, dimensions={0}, use_global_device_ids=true | all-gather | bytes 24000 | tf_op jit(solution)/shard_map/all_gather | solution.py:168
  136.5 11.8 %all-gather.1 = f32[4,2,400]{2,1,0:T(2,128)S(1)} all-gather(f32[1,2,400]{2,1,0:T(2,128)S(1)} %bitcast.232), channel_id=2, replica_groups=mesh['dp'=2,'wide'=4,'narrow'=4] {'narrow'}, dimensions={0}, use_global_device_ids=true | all-gather | bytes 16000 | tf_op jit(solution)/shard_map/all_gather | solution.py:171
  153.6 2.7 convolution_convert_fusion.8
  156.4 5.7 all-gather.15.cloned.1.call-done
  162.0 4.3 fusion.78
  167.7 18.7 %all_to_all.76 = f32[4,128,400]{1,2,0:T(8,128)S(1)} all-to-all(f32[4,128,400]{1,2,0:T(8,128)S(1)} %copy_bitcast_fusion), channel_id=1, replica_groups=mesh['dp'=2,'wide'=4,'narrow'=4] {'wide'}, dimensions={0} | all-to-all | bytes 1638400 | tf_op jit(solution)/shard_map/all_to_all | solution.py:75
  189.8 22.8 %all-gather.19.cloned.1.call-done = bf16[1600,1600]{1,0:T(8,128)(2,1)} async-done(((bf16[200,1600]{1,0:T(8,128)(2,1)}), bf16[1600,1600]{1,0:T(8,128)(2,1)}) %all-gather.19.cloned.1.call-update) | async-done | bytes 5120016 | tf_op jit(solution)/shard_map/all_gather | solution.py:166
  212.7 37.3 %all-gather.17.cloned.1.call-done = bf16[512,1600]{0,1:T(8,128)(2,1)} async-done(((bf16[128,1600]{0,1:T(8,128)(2,1)}), bf16[512,1600]{0,1:T(8,128)(2,1)}) %all-gather.17.cloned.1.call-update) | async-done | bytes 1638416 | tf_op jit(solution)/shard_map/all_gather | solution.py:59
  250.0 7.9 convolution_add_fusion
  257.9 31.1 %all-gather.23.cloned.1.call-done = bf16[512,1600]{0,1:T(8,128)(2,1)} async-done(((bf16[128,1600]{0,1:T(8,128)(2,1)}), bf16[512,1600]{0,1:T(8,128)(2,1)}) %all-gather.23.cloned.1.call-update) | async-done | bytes 1638416 | tf_op jit(solution)/shard_map/all_gather | solution.py:59
  289.0 45.2 %all-gather.21.cloned.1.call-done = bf16[1600,1600]{1,0:T(8,128)(2,1)} async-done(((bf16[200,1600]{1,0:T(8,128)(2,1)}), bf16[1600,1600]{1,0:T(8,128)(2,1)}) %all-gather.21.cloned.1.call-update) | async-done | bytes 5120016 | tf_op jit(solution)/shard_map/all_gather | solution.py:167
  334.3 9.2 %fusion.89 = (f32[1600]{0:T(1024)S(1)}, bf16[512,1600]{0,1:T(8,128)(2,1)S(1)}) fusion(f32[512,1600]{0,1:T(8,128)} %convolution_add_fusion, bf16[1600,1600]{1,0:T(8,128)(2,1)} %all-gather.21.cloned.1.call-done, bf16[512,1600]{0,1:T(8,128)(2,1)} %all-gather.23.cloned.1.call-done), kind=kOutput, calls=%fused_computation.128 | convolution fusion | flops 2637822464 | bytes 11680000 | tf_op jit(solution)/shard_map/dot_general | solution.py:28
  344.7 6.7 convolution_convert_fusion.5
  351.4 3.5 copy.124
  355.2 8.0 convolution_convert_fusion.6
  363.2 3.5 copy.122
  366.8 8.6 %fusion.2 = bf16[1600,1600]{0,1:T(8,128)(2,1)} fusion(bf16[512,1600]{0,1:T(8,128)(2,1)} %all-gather.23.cloned.1.call-done, f32[512,1600]{0,1:T(8,128)} %convolution_add_fusion), kind=kOutput, calls=%fused_computation.5 | convolution fusion | flops 2631372800 | bytes 10035200 | tf_op jit(solution)/shard_map/dot_general | solution.py:28
  375.5 7.5 convolution_convert_fusion.1
  386.3 3.7 reduce-scatter.27.cloned.1.call-done
  391.3 37.8 %reduce-scatter.25.cloned.1.call-done = bf16[128,1600]{1,0:T(8,128)(2,1)} async-done(((bf16[512,1600]{1,0:T(8,128)(2,1)}), bf16[128,1600]{1,0:T(8,128)(2,1)}) %reduce-scatter.25.cloned.1.call-update) | async-done | bytes 409616
  434.3 4.9 convolution_convert_fusion.7
  439.3 3.9 bitcast_convert_fusion
  444.8 4.6 bitcast_convert_fusion.2
  449.4 4.8 bitcast_convert_fusion.1
  456.5 5.0 convolution_convert_fusion.2
  463.5 90.7 %all-reduce.9.cloned.1.call-done = bf16[1600,1600]{0,1:T(8,128)(2,1)} async-done(((bf16[1600,1600]{0,1:T(8,128)(2,1)}), bf16[1600,1600]{0,1:T(8,128)(2,1)}) %all-reduce.9.cloned.1.call-update) | async-done | bytes 5120016
  561.0 59.0 %reduce-scatter.35.cloned.1.call-done = bf16[200,1600]{1,0:T(8,128)(2,1)} async-done(((bf16[1600,1600]{1,0:T(8,128)(2,1)}), bf16[200,1600]{1,0:T(8,128)(2,1)}) %reduce-scatter.35.cloned.1.call-update) | async-done | bytes 640016
  621.0 6.1 multiply_reduce_fusion.1
  628.0 58.3 %reduce-scatter.33.cloned.1.call-done = bf16[200,1600]{1,0:T(8,128)(2,1)} async-done(((bf16[1600,1600]{1,0:T(8,128)(2,1)}), bf16[200,1600]{1,0:T(8,128)(2,1)}) %reduce-scatter.33.cloned.1.call-update) | async-done | bytes 640016
  688.6 6.7 convolution_convert_fusion.4
  695.3 3.5 all-to-all-start.1
  698.9 3.0 convert_element_type.135
  701.9 7.8 all-to-all-done.1
  709.7 3.5 all-to-all-start.3
  714.2 3.0 convert_element_type.132
  717.2 8.4 %all-reduce.4 = (f32[512,1]{0,1:T(1,128)S(1)}, f32[512,1]{0,1:T(1,128)S(1)}) all-reduce(f32[512,1]{0,1:T(1,128)S(1)} %bitcast.245, f32[512,1]{0,1:T(1,128)S(1)} %bitcast.246), channel_id=1, replica_groups=mesh['dp'=2,'wide'=4,'narrow'=4] {'wide'}, use_global_device_ids=true, to_apply=%region_16.17 | all-reduce | flops 1024 | bytes 8192 | tf_op jit(solution)/shard_map/psum | solution.py:32
  726.8 61.2 %all-reduce.11.cloned.1.call-done = (f32[3,1600]{1,0:T(4,128)}, f32[5,1600]{1,0:T(8,128)}, f32[6400]{0:T(1024)}) async-done(((f32[3,1600]{1,0:T(4,128)}, f32[5,1600]{1,0:T(8,128)}, f32[6400]{0:T(1024)}), (f32[3,1600]{1,0:T(4,128)}, f32[5,1600]{1,0:T(8,128)}, f32[6400]{0:T(1024)})) %all-reduce.11.cloned.1.call-update) | async-done | bytes 76816 | tf_op jit(solution)/shard_map/psum | solution.py:256
  794.9 3.9 all_gather.57
  799.9 2.7 all_gather.56
  804.1 2.9 copy.115
  (172 shorter events, 63.9 us)
Async XLA Ops:
  8.0 95.4 %copy-start = (f32[400,1600]{1,0:T(8,128)S(1)}, f32[400,1600]{1,0:T(8,128)}, u32[]{:S(2)}) copy-start(f32[400,1600]{1,0:T(8,128)} %param.26) | copy-start | bytes 7680004
  8.0 56.6 %all-gather.13.cloned.1.call-start = ((), (), s32[]{:S(2)}) async-start(), calls=%async_computation.11 | async-start | bytes 4608000 | tf_op jit(solution)/shard_map/all_gather | solution.py:162
  13.5 4.5 copy-start.2
  15.9 48.7 %copy-start.23 = (f32[400]{0:T(512)S(1)}, f32[400]{0:T(512)}, u32[]{:S(2)}) copy-start(f32[400]{0:T(512)} %param.18) | copy-start | bytes 4804
  15.9 48.7 %copy-start.25 = (f32[400]{0:T(512)S(1)}, f32[400]{0:T(512)}, u32[]{:S(2)}) copy-start(f32[400]{0:T(512)} %param.19) | copy-start | bytes 4804
  18.0 130.7 %reduce-scatter.23.cloned.1.call-start = ((), (), s32[]{:S(2)}) async-start(), calls=%async_computation.20 | async-start | bytes 6225920
  80.3 81.7 %all-gather.15.cloned.1.call-start = ((), (), s32[]{:S(2)}) async-start(), calls=%async_computation.12 | async-start | bytes 5990400 | tf_op jit(solution)/shard_map/all_gather | solution.py:165
  103.3 1.0 copy-start.26
  103.3 109.3 %all-gather.19.cloned.1.call-start = ((), (), s32[]{:S(2)}) async-start(), calls=%async_computation.14 | async-start | bytes 5990400 | tf_op jit(solution)/shard_map/all_gather | solution.py:166
  104.3 9.5 %copy-start.20 = (f32[400]{0:T(512)S(1)}, f32[400]{0:T(512)}, u32[]{:S(2)}) copy-start(f32[400]{0:T(512)} %param.25) | copy-start | bytes 4804
  104.3 9.5 %copy-start.21 = (f32[400]{0:T(512)S(1)}, f32[400]{0:T(512)}, u32[]{:S(2)}) copy-start(f32[400]{0:T(512)} %param.24) | copy-start | bytes 4804
  104.3 9.5 %copy-start.22 = (f32[400]{0:T(512)S(1)}, f32[400]{0:T(512)}, u32[]{:S(2)}) copy-start(f32[400]{0:T(512)} %param.23) | copy-start | bytes 4804
  104.4 32.1 %copy-start.18 = (f32[2,400]{1,0:T(2,128)S(1)}, f32[2,400]{1,0:T(2,128)}, u32[]{:S(2)}) copy-start(f32[2,400]{1,0:T(2,128)} %param.21) | copy-start | bytes 9604
  104.4 44.2 %collective-permute-start = (s32[1,128]{1,0:T(1,128)S(1)}, s32[1,128]{1,0:T(1,128)S(1)}, u32[]{:S(2)}, u32[]{:S(2)}) collective-permute-start(s32[1,128]{1,0:T(1,128)S(1)} %copy-done.26), channel_id=1, source_target_pairs={{0,0},{4,1},{8,2},{12,3},{1,4},{5,5},{9,6},{13,7},{2,8},{6,9},{10,... | collective-permute-start | bytes 1544 | tf_op jit(solution)/shard_map/ppermute | solution.py:159
  109.6 46.8 %all-to-all-start = ((f32[4,128,400]{1,2,0:T(8,128)}), f32[4,128,400]{1,2,0:T(8,128)}, u32[]{:S(2)}, u32[]{:S(2)}) async-start(f32[4,128,400]{1,2,0:T(8,128)} %copy_bitcast_fusion.1), calls=%async_computation | async-start | bytes 1638400 | tf_op jit(solution)/shard_map/all_to_all | solution.py:75
  113.8 136.2 %all-gather.17.cloned.1.call-start = ((), (), s32[]{:S(2)}) async-start(), calls=%async_computation.13 | async-start | bytes 2048000 | tf_op jit(solution)/shard_map/all_gather | solution.py:59
  152.0 4.3 copy-start.5
  152.0 4.3 copy-start.7
  152.0 4.3 copy-start.10
  156.3 5.7 copy-start.12
  166.3 1.3 copy-start.3
  167.6 121.4 %all-gather.23.cloned.1.call-start = ((), (), s32[]{:S(2)}) async-start(), calls=%async_computation.16 | async-start | bytes 2048000 | tf_op jit(solution)/shard_map/all_gather | solution.py:59
  186.5 63.5 %copy-start.24 = (f32[1600]{0:T(1024)S(1)}, f32[1600]{0:T(1024)}, u32[]{:S(2)}) copy-start(f32[1600]{0:T(1024)} %param.27) | copy-start | bytes 19204
  187.3 147.0 %all-gather.21.cloned.1.call-start = ((), (), s32[]{:S(2)}) async-start(), calls=%async_computation.15 | async-start | bytes 5990400 | tf_op jit(solution)/shard_map/all_gather | solution.py:167
  189.6 200.4 %reduce-scatter.27.cloned.1.call-start = ((), (), s32[]{:S(2)}) async-start(), calls=%async_computation.22 | async-start | bytes 2129920
  343.5 1.2 copy-start.28
  355.0 74.1 %reduce-scatter.25.cloned.1.call-start = ((), (), s32[]{:S(2)}) async-start(), calls=%async_computation.21 | async-start | bytes 2129920
  366.8 187.4 %all-reduce.9.cloned.1.call-start = ((), (), s32[]{:S(2)}) async-start(), calls=%async_computation.25 | async-start | bytes 10649600
  375.5 244.5 %reduce-scatter.35.cloned.1.call-start = ((), (), s32[]{:S(2)}) async-start(), calls=%async_computation.27 | async-start | bytes 5990400
  383.0 1.1 copy-start.8
  383.1 237.9 %all-gather.25.cloned.1.call-start = ((), (), s32[]{:S(2)}) async-start(), calls=%async_computation.17 | async-start | bytes 6144000 | tf_op jit(solution)/shard_map/all_gather | solution.py:55
  439.3 4.0 copy-start.11
  443.2 1.6 copy-start.9
  455.3 1.2 copy-start.13
  456.5 229.8 %reduce-scatter.33.cloned.1.call-start = ((), (), s32[]{:S(2)}) async-start(), calls=%async_computation.26 | async-start | bytes 5990400
  461.6 237.3 %all-gather.29.cloned.1.call-start = ((), (), s32[]{:S(2)}) async-start(), calls=%async_computation.19 | async-start | bytes 1996800 | tf_op jit(solution)/shard_map/all_gather | solution.py:207
  463.5 93.6 %copy-start.4 = (f32[400,512]{1,0:T(8,128)S(1)}, f32[400,512]{1,0:T(8,128)}, u32[]{:S(2)}) copy-start(f32[400,512]{1,0:T(8,128)} %param.16) | copy-start | bytes 2457604
  555.8 3.2 copy-start.14
  556.9 2.1 copy-start.15
  557.0 157.3 %all-gather.27.cloned.1.call-start = ((), (), s32[]{:S(2)}) async-start(), calls=%async_computation.18 | async-start | bytes 1996800 | tf_op jit(solution)/shard_map/all_gather | solution.py:207
  557.5 62.5 %copy-start.16 = (f32[6400]{0:T(1024)}, f32[6400]{0:T(1024)S(1)}, u32[]{:S(2)}) copy-start(f32[6400]{0:T(1024)S(1)} %dynamic_update_slice.7) | copy-start | bytes 76804
  620.0 168.0 %all-reduce.11.cloned.1.call-start = ((), (), s32[]{:S(2)}) async-start(), calls=%async_computation.28 | async-start | bytes 217088 | tf_op jit(solution)/shard_map/psum | solution.py:256
  628.0 165.9 %reduce-scatter.31.cloned.1.call-start = ((), (), s32[]{:S(2)}) async-start(), calls=%async_computation.24 | async-start | bytes 1024000
  688.6 111.3 %reduce-scatter.29.cloned.1.call-start = ((), (), s32[]{:S(2)}) async-start(), calls=%async_computation.23 | async-start | bytes 4608000 | tf_op jit(solution)/shard_map/reduce_scatter | solution.py:227
  695.3 14.4 %all-to-all-start.1 = ((f32[128,4,400]{0,2,1:T(8,128)}), f32[128,4,400]{0,2,1:T(8,128)S(1)}, u32[]{:S(2)}, u32[]{:S(2)}) async-start(f32[128,4,400]{0,2,1:T(8,128)} %bitcast.30), calls=%async_computation.1 | async-start | bytes 1638400 | tf_op jit(solution)/shard_map/all_to_all | solution.py:79
  698.9 14.3 %copy-start.19 = (f32[400]{0:T(512)S(1)}, f32[400]{0:T(512)}, u32[]{:S(2)}) copy-start(f32[400]{0:T(512)} %param.29) | copy-start | bytes 4804
  709.7 16.0 %all-to-all-start.3 = ((f32[128,4,400]{0,2,1:T(8,128)}), f32[128,4,400]{0,2,1:T(8,128)S(1)}, u32[]{:S(2)}, u32[]{:S(2)}) async-start(f32[128,4,400]{0,2,1:T(8,128)} %bitcast.38), calls=%async_computation.3 | async-start | bytes 1638400 | tf_op jit(solution)/shard_map/all_to_all | solution.py:79
  804.1 2.9 copy-start.1
  (3 other events, 2.3 us)
Sparse Core Ops, SparseCore 0:
  18.1 46.4 all-gather.12
  80.5 66.6 reduce-scatter.22
  456.6 59.4 all-gather.24
  557.1 10.3 all-gather.28
  620.1 10.3 all-gather.26
  636.4 151.6 all-reduce.10
Sparse Core Ops, SparseCore 1:
  103.4 58.6 all-gather.14
  164.3 48.3 all-gather.18
  214.7 35.3 all-gather.16
  252.2 36.8 all-gather.22
  291.5 42.7 all-gather.20
  355.1 34.9 reduce-scatter.26
  392.8 36.3 reduce-scatter.24
  432.3 121.8 all-reduce.8
  557.4 62.5 reduce-scatter.34
  623.4 62.8 reduce-scatter.32
  689.0 21.4 reduce-scatter.30
  712.9 50.0 reduce-scatter.28
where the time goes:
time: 824 us; the launch traced here: 815 us
  waiting for transfers between devices  499 us (61%)
  matrix products  105 us (13%)
  blocking collectives  93.2 us (11%)
  local copies, waits for them, and re-layouts  59.8 us (7%)
  other arithmetic  23.3 us (3%)
  starting transfers between devices  17.2 us (2%)
  between operations  17.2 us (2%)
    unnamed x25, waiting for transfers between devices  250 us
    all_gather x2, waiting for transfers between devices, gather_narrow(): return lax.all_gather(values, 'narrow', axis=0, tiled=True)  68.5 us
    dot_general x9, matrix products, dot(): lax.dot_general(a, b, (((ca,), (cb,)), ((), ())), preferred_element_type=...  62.2 us
    psum x1, waiting for transfers between devices, local(): lax.psum((token_terms, feature_full, fc_full), ('dp', 'wide', 'narrow'))  61.2 us
    all_gather x1, waiting for transfers between devices, local(): lax.all_gather(own_half(w_proj.astype(BF), 0), ('wide', 'dp'), axis=0, ti...  45.2 us
    all_gather x1, waiting for transfers between devices, local(): wq_all = lax.all_gather(wq_mine, ('narrow', 'dp'), axis=0, tiled=True)  38.4 us
    unnamed x72, local copies, waits for them, and re-layouts  33.5 us
    all_gather x1, waiting for transfers between devices, local(): lax.all_gather(own_half(w_fc.astype(BF), 0), ('wide', 'dp'), axis=0, tile...  22.8 us
  transfers between devices with their start and end apart: 22, of which 13 were waited for; matrix products, arithmetic and copies ran while one was open for 17% of the time, Pallas kernels for 0%

commit v1 on v0

--- a/solution.py
+++ b/solution.py
@@ -10,6 +10,28 @@
 GELU_C = math.sqrt(2.0 / math.pi)
 BF = jnp.bfloat16
 F32 = jnp.float32
+
+
+def in_order(pieces, dim):
+    pieces = jnp.moveaxis(pieces, 0, dim)
+    lengths = pieces.shape
+    return pieces.reshape(*lengths[:dim], lengths[dim] * lengths[dim + 1], *lengths[dim + 2 :])
+
+
+def grow_blocks(x, axis):
+    size = lax.axis_size(axis)
+    pieces = x[None]
+    for level in range(size.bit_length() - 1):
+        bit = 1 << level
+        other = lax.ppermute(pieces, axis, [(i, i ^ bit) for i in range(size)])
+        both = jnp.stack([pieces, other])
+        upper = lax.axis_index(axis) >> level & 1
+        pieces = jnp.where(upper == 0, both, both[::-1]).reshape(-1, *x.shape)
+    return pieces
+
+
+def doubled_up(x, axis, dim):
+    return in_order(grow_blocks(x, axis), dim)
 
 
 def gelu_value(pre_act):
@@ -56,7 +78,7 @@
 
 
 def gather_narrow(values):
-    return lax.all_gather(values, "narrow", axis=0, tiled=True)
+    return doubled_up(values, "narrow", 0)
 
 
 def sum_tokens(partial_value):

time: 824 us -> 733 us (0.89)
  waiting for transfers between devices: 499 us -> 407 us
  blocking collectives: 93.2 us -> 73.4 us
  starting transfers between devices: 17.2 us -> 27.1 us
    all_gather x2 -> x0, waiting for transfers between devices: 68.5 us -> none  [gather_narrow(): return lax.all_gather(values, 'narrow', axis=0, tiled=True)]
    all_gather x1, waiting for transfers between devices: 0.01 us -> 59.9 us  [gather_tokens(): return lax.all_gather(values, 'wide', axis=0, tiled=True)]
    unnamed x25 -> x23, waiting for transfers between devices: 250 us -> 196 us
    ppermute x0 -> x4, waiting for transfers between devices: none -> 50.5 us  [grow_blocks(): other = lax.ppermute(pieces, axis, [(i, i ^ bit) for i in range(size)])]
    all_gather x1, waiting for transfers between devices: 45.2 us -> 2.26 us  [local(): lax.all_gather(own_half(w_proj.astype(BF), 0), ('wide', 'dp'), axis=0, ti...]
    all_gather x1, waiting for transfers between devices: 22.8 us -> 0.03 us  [local(): lax.all_gather(own_half(w_fc.astype(BF), 0), ('wide', 'dp'), axis=0, tile...]
    all_to_all x1 -> x0, blocking collectives: 18.7 us -> none  [to_tokens(): lax.all_to_all(values, 'wide', split_axis=0, concat_axis=1, tiled=True)]
    psum x1, waiting for transfers between devices: 61.2 us -> 43.6 us  [local(): lax.psum((token_terms, feature_full, fc_full), ('dp', 'wide', 'narrow'))]
  transfers between devices with their start and end apart: 22 -> 25, of which waited for: 13 -> 14; matrix products, arithmetic and copies ran while one was open for 17% -> 21% of each run, Pallas kernels for 0% -> 0%
where the time goes in v1:
time: 733 us; the launch traced here: 723 us
  waiting for transfers between devices  407 us (56%)
  matrix products  102 us (14%)
  blocking collectives  73.4 us (10%)
  local copies, waits for them, and re-layouts  65.8 us (9%)
  other arithmetic  30.7 us (4%)
  starting transfers between devices  27.1 us (4%)
  between operations  16.7 us (2%)
    unnamed x23, waiting for transfers between devices  196 us
    all_gather x1, waiting for transfers between devices, gather_tokens(): return lax.all_gather(values, 'wide', axis=0, tiled=True)  59.9 us
    dot_general x9, matrix products, dot(): lax.dot_general(a, b, (((ca,), (cb,)), ((), ())), preferred_element_type=...  59.8 us
    ppermute x4, waiting for transfers between devices, grow_blocks(): other = lax.ppermute(pieces, axis, [(i, i ^ bit) for i in range(size)])  50.5 us
    psum x1, waiting for transfers between devices, local(): lax.psum((token_terms, feature_full, fc_full), ('dp', 'wide', 'narrow'))  43.6 us
    all_gather x1, waiting for transfers between devices, local(): wq_all = lax.all_gather(wq_mine, ('narrow', 'dp'), axis=0, tiled=True)  38.4 us
    unnamed x74, local copies, waits for them, and re-layouts  31.5 us
    all_gather x1, blocking collectives, local(): lax.all_gather(jnp.stack([b_out, ln2_gain, ln2_shift]), 'wide', axis=1, t...  22.2 us
  transfers between devices with their start and end apart: 25, of which 14 were waited for; matrix products, arithmetic and copies ran while one was open for 21% of the time, Pallas kernels for 0%

profile of v1, /device:TPU:9, one launch (start us, length us, event | category | flops | bytes accessed | tf_op | source)
XLA Modules:
  0.0 723.2 jit_solution(10309658176046283339)
XLA Ops:
  8.1 3.0 convert_element_type.121
  18.2 7.9 %all-reduce.5 = (f32[512,1]{0,1:T(1,128)S(1)}, f32[512,1]{0,1:T(1,128)S(1)}) all-reduce(f32[512,1]{0,1:T(1,128)S(1)} %bitcast.249, f32[512,1]{0,1:T(1,128)S(1)} %bitcast.248), channel_id=1, replica_groups=mesh['dp'=2,'wide'=4,'narrow'=4] {'wide'}, use_global_device_ids=true, to_apply=%region_3.4 | all-reduce | flops 1024 | bytes 8192 | tf_op jit(solution)/shard_map/psum | solution.py:54
  26.2 38.4 %all-gather.11.cloned.1.call-done = bf16[1600,1200]{1,0:T(8,128)(2,1)} async-done(((bf16[200,1200]{1,0:T(8,128)(2,1)}), bf16[1600,1200]{1,0:T(8,128)(2,1)}) %all-gather.11.cloned.1.call-update) | async-done | bytes 3840016 | tf_op jit(solution)/shard_map/all_gather | solution.py:184
  64.6 8.2 %convolution_convert_fusion.3 = bf16[512,4,1200]{0,2,1:T(8,128)(2,1)} fusion(bf16[4,400,1200]{2,1,0:T(8,128)(2,1)} %bitcast.275, f32[400,512]{1,0:T(8,128)S(1)} %copy-done.2, f32[400]{0:T(512)S(1)} %copy-done.28, f32[400]{0:T(512)S(1)} %copy-done.25, f32[512]{0:T(512)S(1)} %bitcast.256, f32[512]{0:T(512)S(1)} %bitcast.252), kind=kOutput, calls=%fused_computation.5 | convolution fusion | flops 1969561600 | bytes 9581696 | tf_op jit(solution)/shard_map/tk,nkc->tnc/dot_general | solution.py:203
  72.8 7.5 %copy.138 = bf16[512,4800]{1,0:T(8,128)(2,1)} copy(bf16[512,4800]{0,1:T(8,128)(2,1)} %bitcast.209) | data formatting | bytes 9830400
  83.9 17.1 %all_gather.42 = bf16[200,1600]{0,1:T(8,128)(2,1)} all-gather(bf16[200,400]{0,1:T(8,128)(2,1)} %copy.142), channel_id=1, replica_groups=mesh['dp'=2,'wide'=4,'narrow'=4] {'narrow'}, dimensions={1}, use_global_device_ids=true | all-gather | bytes 800000 | tf_op jit(solution)/shard_map/all_gather | solution.py:186
  107.7 3.5 all-to-all-start.2
  111.2 4.4 collective-permute-start
  115.6 11.5 %all-gather.1 = f32[4,2,400]{2,1,0:T(2,128)S(1)} all-gather(f32[1,2,400]{2,1,0:T(2,128)S(1)} %bitcast.260), channel_id=2, replica_groups=mesh['dp'=2,'wide'=4,'narrow'=4] {'narrow'}, dimensions={0}, use_global_device_ids=true | all-gather | bytes 16000 | tf_op jit(solution)/shard_map/all_gather | solution.py:193
  128.1 2.9 all-to-all-done.2
  131.1 4.2 all-to-all-start
  135.7 22.2 %all-gather.2 = f32[4,400,3]{1,2,0:T(4,128)S(1)} all-gather(f32[1,400,3]{1,2,0:T(4,128)S(1)} %maximum_bitcast_fusion.1), channel_id=1, replica_groups=mesh['dp'=2,'wide'=4,'narrow'=4] {'wide'}, dimensions={0}, use_global_device_ids=true | all-gather | bytes 24000 | tf_op jit(solution)/shard_map/all_gather | solution.py:190
  171.8 4.4 fusion.80
  177.3 22.3 %collective-permute-done.1 = bf16[1,128,1600]{1,2,0:T(8,128)(2,1)S(1)} collective-permute-done((bf16[1,128,1600]{1,2,0:T(8,128)(2,1)S(1)}, bf16[1,128,1600]{1,2,0:T(8,128)(2,1)S(1)}, u32[]{:S(2)}, u32[]{:S(2)}) %collective-permute-start.1) | collective-permute-done | bytes 409632 | tf_op jit(solution)/shard_map/ppermute | solution.py:26
  201.0 3.5 collective-permute-start.2
  207.3 3.7 copy.114
  210.9 28.2 %collective-permute-done.2 = bf16[2,128,1600]{1,2,0:T(8,128)(2,1)} collective-permute-done((bf16[2,128,1600]{1,2,0:T(8,128)(2,1)}, bf16[2,128,1600]{1,2,0:T(8,128)(2,1)}, u32[]{:S(2)}, u32[]{:S(2)}) %collective-permute-start.2) | collective-permute-done | bytes 819232 | tf_op jit(solution)/shard_map/ppermute | solution.py:26
  242.0 3.7 copy.111
  245.7 8.0 %convolution_add_fusion = f32[512,1600]{0,1:T(8,128)} fusion(bf16[512,1600]{1,0:T(8,128)(2,1)} %bitcast.219, bf16[1600,1600]{1,0:T(8,128)(2,1)} %all-gather.15.cloned.1.call-done, f32[1600]{0:T(1024)S(1)} %copy-done.27), kind=kOutput, calls=%fused_computation.16 | convolution fusion | flops 2622259200 | bytes 10041600 | tf_op jit(solution)/shard_map/dot_general | solution.py:50
  256.0 9.4 %fusion.91 = (f32[1600]{0:T(1024)S(1)}, bf16[512,1600]{0,1:T(8,128)(2,1)S(1)}) fusion(f32[512,1600]{0,1:T(8,128)} %convolution_add_fusion, bf16[512,1600]{1,0:T(8,128)(2,1)} %bitcast.217, bf16[1600,1600]{1,0:T(8,128)(2,1)} %all-gather.17.cloned.1.call-done), kind=kOutput, calls=%fused_computation.138 | convolution fusion | flops 2637822464 | bytes 11680000 | tf_op jit(solution)/shard_map/dot_general | solution.py:50
  266.5 4.2 convolution_convert_fusion.5
  270.7 3.5 copy.132
  274.6 8.0 %convolution_convert_fusion.6 = bf16[512,1600]{0,1:T(8,128)(2,1)} fusion(bf16[1600,1600]{1,0:T(8,128)(2,1)} %all-gather.17.cloned.1.call-done, f32[512,1600]{0,1:T(8,128)} %convolution_add_fusion), kind=kOutput, calls=%fused_computation.18 | convolution fusion | flops 2629632000 | bytes 10035200 | tf_op jit(solution)/shard_map/dot_general | solution.py:50
  282.5 3.6 copy.130
  286.2 7.6 %convolution_convert_fusion.1 = bf16[1600,1600]{1,0:T(8,128)(2,1)} fusion(bf16[512,1600]{1,0:T(8,128)(2,1)} %bitcast.220, bf16[512,1600]{0,1:T(8,128)(2,1)} %copy-done.30), kind=kOutput, calls=%fused_computation.3 | convolution fusion | flops 2624000000 | bytes 8396800 | tf_op jit(solution)/shard_map/dot_general | solution.py:50
  293.9 8.2 %convolution_convert_fusion = bf16[1600,1600]{1,0:T(8,128)(2,1)} fusion(bf16[512,1600]{1,0:T(8,128)(2,1)} %bitcast.218, f32[512,1600]{0,1:T(8,128)} %convolution_add_fusion), kind=kOutput, calls=%fused_computation.2 | convolution fusion | flops 2631372800 | bytes 10035200 | tf_op jit(solution)/shard_map/dot_general | solution.py:50
  305.4 4.1 reduce-scatter.29.cloned.1.call-done
  310.7 37.4 %reduce-scatter.27.cloned.1.call-done = bf16[128,1600]{1,0:T(8,128)(2,1)} async-done(((bf16[512,1600]{1,0:T(8,128)(2,1)}), bf16[128,1600]{1,0:T(8,128)(2,1)}) %reduce-scatter.27.cloned.1.call-update) | async-done | bytes 409616
  353.3 4.9 convolution_convert_fusion.7
  358.2 3.7 bitcast_convert_fusion
  363.5 5.1 bitcast_convert_fusion.1
  368.6 4.8 bitcast_convert_fusion.2
  375.8 5.0 convolution_convert_fusion.2
  380.9 33.7 %reduce-scatter.37.cloned.1.call-done = bf16[200,1600]{1,0:T(8,128)(2,1)} async-done(((bf16[1600,1600]{1,0:T(8,128)(2,1)}), bf16[200,1600]{1,0:T(8,128)(2,1)}) %reduce-scatter.37.cloned.1.call-update) | async-done | bytes 640016
  418.6 61.7 %reduce-scatter.39.cloned.1.call-done = bf16[200,1600]{1,0:T(8,128)(2,1)} async-done(((bf16[1600,1600]{1,0:T(8,128)(2,1)}), bf16[200,1600]{1,0:T(8,128)(2,1)}) %reduce-scatter.39.cloned.1.call-update) | async-done | bytes 640016
  481.3 59.9 %all-gather.19.cloned.1.call-done = bf16[512,4,1200]{0,2,1:T(8,128)(2,1)} async-done(((bf16[128,4,1200]{0,2,1:T(8,128)(2,1)}), bf16[512,4,1200]{0,2,1:T(8,128)(2,1)}) %all-gather.19.cloned.1.call-update) | async-done | bytes 4915216 | tf_op jit(solution)/shard_map/all_gather | solution.py:77
  541.2 6.1 multiply_reduce_fusion.1
  548.3 58.9 %reduce-scatter.35.cloned.1.call-done = bf16[200,1600]{1,0:T(8,128)(2,1)} async-done(((bf16[1600,1600]{1,0:T(8,128)(2,1)}), bf16[200,1600]{1,0:T(8,128)(2,1)}) %reduce-scatter.35.cloned.1.call-update) | async-done | bytes 640016
  609.5 6.7 convolution_convert_fusion.4
  616.2 3.5 all-to-all-start.1
  619.7 10.8 %all-to-all-done.1 = f32[128,4,400]{0,2,1:T(8,128)S(1)} async-done(((f32[128,4,400]{0,2,1:T(8,128)}), f32[128,4,400]{0,2,1:T(8,128)S(1)}, u32[]{:S(2)}, u32[]{:S(2)}) %all-to-all-start.1) | async-done | bytes 819232 | tf_op jit(solution)/shard_map/all_to_all | solution.py:101
  630.5 3.5 all-to-all-start.3
  635.0 3.0 convert_element_type.151
  638.0 3.0 convert_element_type.153
  641.0 8.1 %all-reduce.4 = (f32[512,1]{0,1:T(1,128)S(1)}, f32[512,1]{0,1:T(1,128)S(1)}) all-reduce(f32[512,1]{0,1:T(1,128)S(1)} %bitcast.273, f32[512,1]{0,1:T(1,128)S(1)} %bitcast.274), channel_id=1, replica_groups=mesh['dp'=2,'wide'=4,'narrow'=4] {'wide'}, use_global_device_ids=true, to_apply=%region_16.17 | all-reduce | flops 1024 | bytes 8192 | tf_op jit(solution)/shard_map/psum | solution.py:54
  650.3 43.6 %all-reduce.8.cloned.1.call-done = (f32[3,1600]{1,0:T(4,128)}, f32[5,1600]{1,0:T(8,128)}, f32[6400]{0:T(1024)}) async-done(((f32[3,1600]{1,0:T(4,128)}, f32[5,1600]{1,0:T(8,128)}, f32[6400]{0:T(1024)}), (f32[3,1600]{1,0:T(4,128)}, f32[5,1600]{1,0:T(8,128)}, f32[6400]{0:T(1024)})) %all-reduce.8.cloned.1.call-update) | async-done | bytes 76816 | tf_op jit(solution)/shard_map/psum | solution.py:278
  700.7 3.8 all_gather.49
  712.5 2.9 copy.123
  (187 shorter events, 83.2 us)
Async XLA Ops:
  8.0 95.3 %copy-start = (f32[400,1600]{1,0:T(8,128)S(1)}, f32[400,1600]{1,0:T(8,128)}, u32[]{:S(2)}) copy-start(f32[400,1600]{1,0:T(8,128)} %param.26) | copy-start | bytes 7680004
  8.0 56.6 %all-gather.11.cloned.1.call-start = ((), (), s32[]{:S(2)}) async-start(), calls=%async_computation.12 | async-start | bytes 4608000 | tf_op jit(solution)/shard_map/all_gather | solution.py:184
  13.5 4.5 copy-start.2
  15.9 48.7 %copy-start.25 = (f32[400]{0:T(512)S(1)}, f32[400]{0:T(512)}, u32[]{:S(2)}) copy-start(f32[400]{0:T(512)} %param.18) | copy-start | bytes 4804
  15.9 48.7 %copy-start.28 = (f32[400]{0:T(512)S(1)}, f32[400]{0:T(512)}, u32[]{:S(2)}) copy-start(f32[400]{0:T(512)} %param.19) | copy-start | bytes 4804
  18.0 144.5 %reduce-scatter.25.cloned.1.call-start = ((), (), s32[]{:S(2)}) async-start(), calls=%async_computation.19 | async-start | bytes 6225920
  80.3 91.4 %all-gather.13.cloned.1.call-start = ((), (), s32[]{:S(2)}) async-start(), calls=%async_computation.13 | async-start | bytes 5990400 | tf_op jit(solution)/shard_map/all_gather | solution.py:187
  103.3 142.4 %all-gather.15.cloned.1.call-start = ((), (), s32[]{:S(2)}) async-start(), calls=%async_computation.14 | async-start | bytes 5990400 | tf_op jit(solution)/shard_map/all_gather | solution.py:188
  104.3 2.4 copy-start.3
  104.3 151.7 %all-gather.17.cloned.1.call-start = ((), (), s32[]{:S(2)}) async-start(), calls=%async_computation.15 | async-start | bytes 5990400 | tf_op jit(solution)/shard_map/all_gather | solution.py:189
  106.7 4.5 copy-start.29
  106.7 8.9 %copy-start.20 = (f32[2,400]{1,0:T(2,128)S(1)}, f32[2,400]{1,0:T(2,128)}, u32[]{:S(2)}) copy-start(f32[2,400]{1,0:T(2,128)} %param.21) | copy-start | bytes 9604
  107.7 23.4 %all-to-all-start.2 = ((f32[4,128,400]{1,2,0:T(8,128)}), f32[4,128,400]{1,2,0:T(8,128)S(1)}, u32[]{:S(2)}, u32[]{:S(2)}) async-start(f32[4,128,400]{1,2,0:T(8,128)} %copy_bitcast_fusion), calls=%async_computation.2 | async-start | bytes 1638400 | tf_op jit(solution)/shard_map/all_to_all | solution.py:97
  111.2 47.1 %collective-permute-start = (s32[1,128]{1,0:T(1,128)S(1)}, s32[1,128]{1,0:T(1,128)S(1)}, u32[]{:S(2)}, u32[]{:S(2)}) collective-permute-start(s32[1,128]{1,0:T(1,128)S(1)} %copy-done.29), channel_id=1, source_target_pairs={{0,0},{4,1},{8,2},{12,3},{1,4},{5,5},{9,6},{13,7},{2,8},{6,9},{10,... | collective-permute-start | bytes 1544 | tf_op jit(solution)/shard_map/ppermute | solution.py:181
  128.1 7.6 %copy-start.22 = (f32[400]{0:T(512)S(1)}, f32[400]{0:T(512)}, u32[]{:S(2)}) copy-start(f32[400]{0:T(512)} %param.25) | copy-start | bytes 4804
  128.1 7.6 %copy-start.23 = (f32[400]{0:T(512)S(1)}, f32[400]{0:T(512)}, u32[]{:S(2)}) copy-start(f32[400]{0:T(512)} %param.24) | copy-start | bytes 4804
  128.1 7.6 %copy-start.24 = (f32[400]{0:T(512)S(1)}, f32[400]{0:T(512)}, u32[]{:S(2)}) copy-start(f32[400]{0:T(512)} %param.23) | copy-start | bytes 4804
  131.1 40.7 %all-to-all-start = ((f32[4,128,400]{1,2,0:T(8,128)}), f32[4,128,400]{1,2,0:T(8,128)}, u32[]{:S(2)}, u32[]{:S(2)}) async-start(f32[4,128,400]{1,2,0:T(8,128)} %copy_bitcast_fusion.1), calls=%async_computation | async-start | bytes 1638400 | tf_op jit(solution)/shard_map/all_to_all | solution.py:97
  135.3 174.2 %reduce-scatter.29.cloned.1.call-start = ((), (), s32[]{:S(2)}) async-start(), calls=%async_computation.21 | async-start | bytes 2129920
  135.4 23.0 %collective-permute-start.3 = (bf16[1,128,1600]{1,2,0:T(8,128)(2,1)S(1)}, bf16[1,128,1600]{1,2,0:T(8,128)(2,1)S(1)}, u32[]{:S(2)}, u32[]{:S(2)}) collective-permute-start(bf16[1,128,1600]{1,2,0:T(8,128)(2,1)S(1)} %bitcast.231), channel_id=1, source_target_pairs={{0,1},{1,0},{2,3},{3,2},{4,5},{5,4},{6,7},{7,6},{8,9},{9,8},{10,11... | collective-permute-start | bytes 1228808 | tf_op jit(solution)/shard_map/ppermute | solution.py:26
  159.9 44.6 %collective-permute-start.4 = (bf16[2,128,1600]{1,2,0:T(8,128)(2,1)}, bf16[2,128,1600]{1,2,0:T(8,128)(2,1)}, u32[]{:S(2)}, u32[]{:S(2)}) collective-permute-start(bf16[2,128,1600]{1,2,0:T(8,128)(2,1)} %get-tuple-element.96), channel_id=1, source_target_pairs={{0,2},{1,3},{2,0},{3,1},{4,6},{5,7},{6,4},{7,5},{8,10},{9,11},{10,... | collective-permute-start | bytes 2457608 | tf_op jit(solution)/shard_map/ppermute | solution.py:26
  166.6 5.1 copy-start.7
  171.7 4.5 copy-start.14
  176.7 22.8 %collective-permute-start.1 = (bf16[1,128,1600]{1,2,0:T(8,128)(2,1)S(1)}, bf16[1,128,1600]{1,2,0:T(8,128)(2,1)S(1)}, u32[]{:S(2)}, u32[]{:S(2)}) collective-permute-start(bf16[1,128,1600]{1,2,0:T(8,128)(2,1)S(1)} %fusion.125), channel_id=1, source_target_pairs={{0,1},{1,0},{2,3},{3,2},{4,5},{5,4},{6,7},{7,6},{8,9},{9,8},{10,11... | collective-permute-start | bytes 1228808 | tf_op jit(solution)/shard_map/ppermute | solution.py:26
  199.5 5.0 copy-start.5
  201.0 38.2 %collective-permute-start.2 = (bf16[2,128,1600]{1,2,0:T(8,128)(2,1)}, bf16[2,128,1600]{1,2,0:T(8,128)(2,1)}, u32[]{:S(2)}, u32[]{:S(2)}) collective-permute-start(bf16[2,128,1600]{1,2,0:T(8,128)(2,1)} %get-tuple-element.98), channel_id=1, source_target_pairs={{0,2},{1,3},{2,0},{3,1},{4,6},{5,7},{6,4},{7,5},{8,10},{9,11},{10,... | collective-permute-start | bytes 2457608 | tf_op jit(solution)/shard_map/ppermute | solution.py:26
  207.3 31.9 %copy-start.6 = (bf16[1,2,128,1600]{2,3,1,0:T(8,128)(2,1)S(1)}, bf16[1,2,128,1600]{2,3,1,0:T(8,128)(2,1)}, u32[]{:S(2)}) copy-start(bf16[1,2,128,1600]{2,3,1,0:T(8,128)(2,1)} %get-tuple-element.97) | copy-start | bytes 2457604
  242.0 3.8 copy-start.27
  256.0 10.5 %copy-start.26 = (bf16[1600,1600]{1,0:T(8,128)(2,1)S(1)}, bf16[1600,1600]{1,0:T(8,128)(2,1)}, u32[]{:S(2)}) copy-start(bf16[1600,1600]{1,0:T(8,128)(2,1)} %all-gather.15.cloned.1.call-done) | copy-start | bytes 15360004
  274.3 73.8 %reduce-scatter.27.cloned.1.call-start = ((), (), s32[]{:S(2)}) async-start(), calls=%async_computation.20 | async-start | bytes 2129920
  286.1 128.5 %reduce-scatter.37.cloned.1.call-start = ((), (), s32[]{:S(2)}) async-start(), calls=%async_computation.25 | async-start | bytes 5990400
  293.8 186.5 %reduce-scatter.39.cloned.1.call-start = ((), (), s32[]{:S(2)}) async-start(), calls=%async_computation.26 | async-start | bytes 5990400
  302.1 239.1 %all-gather.19.cloned.1.call-start = ((), (), s32[]{:S(2)}) async-start(), calls=%async_computation.16 | async-start | bytes 6144000 | tf_op jit(solution)/shard_map/all_gather | solution.py:77
  358.2 3.7 copy-start.13
  375.7 231.4 %reduce-scatter.35.cloned.1.call-start = ((), (), s32[]{:S(2)}) async-start(), calls=%async_computation.24 | async-start | bytes 5990400
  380.8 33.9 %copy-start.4 = (f32[400,512]{1,0:T(8,128)S(1)}, f32[400,512]{1,0:T(8,128)}, u32[]{:S(2)}) copy-start(f32[400,512]{1,0:T(8,128)} %param.16) | copy-start | bytes 2457604
  380.9 35.8 %copy-start.16 = (f32[25,64,128]{2,1,0:T(8,128)S(1)}, f32[25,64,128]{2,1,0:T(8,128)}, u32[]{:S(2)}) copy-start(f32[25,64,128]{2,1,0:T(8,128)} %get-tuple-element.115) | copy-start | bytes 2457604
  380.9 35.8 %copy-start.17 = (f32[25,64,128]{2,1,0:T(8,128)S(1)}, f32[25,64,128]{2,1,0:T(8,128)}, u32[]{:S(2)}) copy-start(f32[25,64,128]{2,1,0:T(8,128)} %get-tuple-element.117) | copy-start | bytes 2457604
  380.9 254.1 %all-gather.21.cloned.1.call-start = ((), (), s32[]{:S(2)}) async-start(), calls=%async_computation.17 | async-start | bytes 1996800 | tf_op jit(solution)/shard_map/all_gather | solution.py:229
  414.6 223.4 %all-gather.23.cloned.1.call-start = ((), (), s32[]{:S(2)}) async-start(), calls=%async_computation.18 | async-start | bytes 1996800 | tf_op jit(solution)/shard_map/all_gather | solution.py:229
  415.2 65.2 %copy-start.18 = (f32[6400]{0:T(1024)}, f32[6400]{0:T(1024)S(1)}, u32[]{:S(2)}) copy-start(f32[6400]{0:T(1024)S(1)} %dynamic_update_slice.7) | copy-start | bytes 76804
  480.4 213.5 %all-reduce.8.cloned.1.call-start = ((), (), s32[]{:S(2)}) async-start(), calls=%async_computation.27 | async-start | bytes 217088 | tf_op jit(solution)/shard_map/psum | solution.py:278
  548.2 151.4 %reduce-scatter.33.cloned.1.call-start = ((), (), s32[]{:S(2)}) async-start(), calls=%async_computation.23 | async-start | bytes 1024000
  609.4 98.8 %reduce-scatter.31.cloned.1.call-start = ((), (), s32[]{:S(2)}) async-start(), calls=%async_computation.22 | async-start | bytes 4608000 | tf_op jit(solution)/shard_map/reduce_scatter | solution.py:249
  616.2 17.8 %copy-start.21 = (f32[400]{0:T(512)S(1)}, f32[400]{0:T(512)}, u32[]{:S(2)}) copy-start(f32[400]{0:T(512)} %param.29) | copy-start | bytes 4804
  616.2 14.3 %all-to-all-start.1 = ((f32[128,4,400]{0,2,1:T(8,128)}), f32[128,4,400]{0,2,1:T(8,128)S(1)}, u32[]{:S(2)}, u32[]{:S(2)}) async-start(f32[128,4,400]{0,2,1:T(8,128)} %bitcast.38), calls=%async_computation.1 | async-start | bytes 1638400 | tf_op jit(solution)/shard_map/all_to_all | solution.py:101
  630.5 18.6 %all-to-all-start.3 = ((f32[128,4,400]{0,2,1:T(8,128)}), f32[128,4,400]{0,2,1:T(8,128)S(1)}, u32[]{:S(2)}, u32[]{:S(2)}) async-start(f32[128,4,400]{0,2,1:T(8,128)} %bitcast.51), calls=%async_computation.3 | async-start | bytes 1638400 | tf_op jit(solution)/shard_map/all_to_all | solution.py:101
  712.5 2.9 copy-start.1
  (8 other events, 9.9 us)
Sparse Core Ops, SparseCore 0:
  18.1 46.4 all-gather.10
  80.5 74.4 reduce-scatter.24
  274.4 35.0 reduce-scatter.28
  311.7 36.3 reduce-scatter.26
  351.3 63.2 reduce-scatter.36
  417.9 62.4 reduce-scatter.38
  482.7 58.4 all-gather.18
  544.6 62.4 reduce-scatter.34
  608.7 10.4 all-gather.20
  620.6 10.6 all-gather.22
  634.1 21.9 reduce-scatter.32
  658.3 49.9 reduce-scatter.30
Sparse Core Ops, SparseCore 1:
  103.4 66.6 all-gather.12
  171.8 41.2 all-gather.14
  214.8 41.2 all-gather.16
  548.3 145.5 all-reduce.7
